TPU v7x, 32 devices: a whole 2x2x4 slice. The times are simulated.
32 devices in a mesh: batch: 8 (over y, x, core), cols: 4 (over z).
Axes of the slice: x: 2, y: 2, z: 4, core: 2. Of those that a mesh axis runs over, the one named last changes fastest.
Arguments:
- grad_up: float32 [8, 1024, 4096], P('batch', None, 'cols'), may hold values from -0.875 to 0.875
- grad_down: float32 [8, 4096, 1024], P('batch', 'cols'), may hold values from -0.875 to 0.875
- grad_query: float32 [8, 1024, 1024], P('batch', None, 'cols'), may hold values from -0.875 to 0.875
- grad_key: float32 [8, 1024, 1024], P('batch', None, 'cols'), may hold values from -0.875 to 0.875
- grad_value: float32 [8, 1024, 1024], P('batch', None, 'cols'), may hold values from -0.875 to 0.875
- grad_mixed: float32 [8, 1024, 1024], P('batch', 'cols'), may hold values from -0.875 to 0.875
- grad_norm: float32 [8, 1024], P('batch'), may hold values from -8 to 8
- weight_up: float32 [1024, 4096], P('batch', 'cols'), may hold values from -0.1875 to 0.1875
- weight_down: float32 [4096, 1024], P('cols', 'batch'), may hold values from -0.09375 to 0.09375
- weight_query: float32 [1024, 1024], P('batch', 'cols'), may hold values from -0.1875 to 0.1875
- weight_key: float32 [1024, 1024], P('batch', 'cols'), may hold values from -0.1875 to 0.1875
- weight_value: float32 [1024, 1024], P('batch', 'cols'), may hold values from -0.1875 to 0.1875
- weight_mixed: float32 [1024, 1024], P('cols', 'batch'), may hold values from -0.1875 to 0.1875
- weight_norm: float32 [1024], P('batch'), may hold values from 0.25 to 1.75
- moment_up: float32 [1024, 4096], P('batch', 'cols'), may hold values from -1.75 to 1.75
- moment_down: float32 [4096, 1024], P('cols', 'batch'), may hold values from -1.75 to 1.75
- moment_query: float32 [1024, 1024], P('batch', 'cols'), may hold values from -1.75 to 1.75
- moment_key: float32 [1024, 1024], P('batch', 'cols'), may hold values from -1.75 to 1.75
- moment_value: float32 [1024, 1024], P('batch', 'cols'), may hold values from -1.75 to 1.75
- moment_mixed: float32 [1024, 1024], P('cols', 'batch'), may hold values from -1.75 to 1.75
- moment_norm: float32 [1024], P('batch'), may hold values from -1.75 to 1.75
Outputs:
- copy_up: bfloat16 [1024, 4096], P(None, 'cols')
- copy_down: bfloat16 [4096, 1024], P('cols')
- copy_query: bfloat16 [1024, 1024], P(None, 'cols')
- copy_key: bfloat16 [1024, 1024], P(None, 'cols')
- copy_value: bfloat16 [1024, 1024], P(None, 'cols')
- copy_mixed: bfloat16 [1024, 1024], P('cols')
- copy_norm: bfloat16 [1024], replicated
- new_up: float32 [1024, 4096], P('batch', 'cols')
- new_down: float32 [4096, 1024], P('cols', 'batch')
- new_query: float32 [1024, 1024], P('batch', 'cols')
- new_key: float32 [1024, 1024], P('batch', 'cols')
- new_value: float32 [1024, 1024], P('batch', 'cols')
- new_mixed: float32 [1024, 1024], P('cols', 'batch')
- new_norm: float32 [1024], P('batch')
- state_new_up: float32 [1024, 4096], P('batch', 'cols')
- state_new_down: float32 [4096, 1024], P('cols', 'batch')
- state_new_query: float32 [1024, 1024], P('batch', 'cols')
- state_new_key: float32 [1024, 1024], P('batch', 'cols')
- state_new_value: float32 [1024, 1024], P('batch', 'cols')
- state_new_mixed: float32 [1024, 1024], P('cols', 'batch')
- state_new_norm: float32 [1024], P('batch')
All inputs are finite; a program needn't handle non-finite values.
Results may differ from a plain program's by a relative error of at most 0.008.
Values may be sent and summed in bfloat16 or wider, within the bound.
A program may use at most 64 MiB of HBM per device.

v0:
```python
import jax
import jax.numpy as jnp
from jax import lax
from jax.sharding import PartitionSpec as P

learn_rate = 0.1
hold_rate = 0.7


def body(
    grad_up,
    grad_down,
    grad_query,
    grad_key,
    grad_value,
    grad_mixed,
    grad_norm,
    weight_up,
    weight_down,
    weight_query,
    weight_key,
    weight_value,
    weight_mixed,
    weight_norm,
    moment_up,
    moment_down,
    moment_query,
    moment_key,
    moment_value,
    moment_mixed,
    moment_norm,
):
    mean_up, mean_down, mean_query, mean_key, mean_value, mean_mixed = (
        lax.psum_scatter(
            grad_up[0].astype(jnp.bfloat16), "batch", scatter_dimension=0, tiled=True
        ).astype(jnp.float32),
        lax.psum_scatter(
            grad_down[0].astype(jnp.bfloat16), "batch", scatter_dimension=1, tiled=True
        ).astype(jnp.float32),
        lax.psum_scatter(
            grad_query[0].astype(jnp.bfloat16), "batch", scatter_dimension=0, tiled=True
        ).astype(jnp.float32),
        lax.psum_scatter(
            grad_key[0].astype(jnp.bfloat16), "batch", scatter_dimension=0, tiled=True
        ).astype(jnp.float32),
        lax.psum_scatter(
            grad_value[0].astype(jnp.bfloat16), "batch", scatter_dimension=0, tiled=True
        ).astype(jnp.float32),
        lax.psum_scatter(
            grad_mixed[0].astype(jnp.bfloat16), "batch", scatter_dimension=1, tiled=True
        ).astype(jnp.float32),
    )
    whole_norm = lax.psum(grad_norm[0], "batch")
    place = lax.axis_index("batch")
    mean_norm = lax.dynamic_slice_in_dim(
        whole_norm, place * weight_norm.shape[0], weight_norm.shape[0]
    )
    mean_rate = lax.axis_size("batch") ** (-0.5)
    mean_up = mean_up * mean_rate
    mean_down = mean_down * mean_rate
    mean_query = mean_query * mean_rate
    mean_key = mean_key * mean_rate
    mean_value = mean_value * mean_rate
    mean_mixed = mean_mixed * mean_rate
    mean_norm = mean_norm * mean_rate
    state_new_up = hold_rate * moment_up + mean_up
    new_up = weight_up - learn_rate * state_new_up
    state_new_down = hold_rate * moment_down + mean_down
    new_down = weight_down - learn_rate * state_new_down
    state_new_query = hold_rate * moment_query + mean_query
    new_query = weight_query - learn_rate * state_new_query
    state_new_key = hold_rate * moment_key + mean_key
    new_key = weight_key - learn_rate * state_new_key
    state_new_value = hold_rate * moment_value + mean_value
    new_value = weight_value - learn_rate * state_new_value
    state_new_mixed = hold_rate * moment_mixed + mean_mixed
    new_mixed = weight_mixed - learn_rate * state_new_mixed
    state_new_norm = hold_rate * moment_norm + mean_norm
    new_norm = weight_norm - learn_rate * state_new_norm
    copy_up, copy_down, copy_query, copy_key, copy_value, copy_mixed, copy_norm = (
        lax.all_gather(new_up.astype(jnp.bfloat16), "batch", axis=0, tiled=True),
        lax.all_gather(new_down.astype(jnp.bfloat16), "batch", axis=1, tiled=True),
        lax.all_gather(new_query.astype(jnp.bfloat16), "batch", axis=0, tiled=True),
        lax.all_gather(new_key.astype(jnp.bfloat16), "batch", axis=0, tiled=True),
        lax.all_gather(new_value.astype(jnp.bfloat16), "batch", axis=0, tiled=True),
        lax.all_gather(new_mixed.astype(jnp.bfloat16), "batch", axis=1, tiled=True),
        lax.all_gather(new_norm.astype(jnp.bfloat16), "batch", axis=0, tiled=True),
    )
    return (
        copy_up,
        copy_down,
        copy_query,
        copy_key,
        copy_value,
        copy_mixed,
        copy_norm,
        new_up,
        new_down,
        new_query,
        new_key,
        new_value,
        new_mixed,
        new_norm,
        state_new_up,
        state_new_down,
        state_new_query,
        state_new_key,
        state_new_value,
        state_new_mixed,
        state_new_norm,
    )


def solution(mesh):
    in_specs = (
        P("batch", None, "cols"),
        P("batch", "cols", None),
        P("batch", None, "cols"),
        P("batch", None, "cols"),
        P("batch", None, "cols"),
        P("batch", "cols", None),
        P("batch", None),
        P("batch", "cols"),
        P("cols", "batch"),
        P("batch", "cols"),
        P("batch", "cols"),
        P("batch", "cols"),
        P("cols", "batch"),
        P("batch"),
        P("batch", "cols"),
        P("cols", "batch"),
        P("batch", "cols"),
        P("batch", "cols"),
        P("batch", "cols"),
        P("cols", "batch"),
        P("batch"),
    )
    out_specs = (
        P(None, "cols"),
        P("cols", None),
        P(None, "cols"),
        P(None, "cols"),
        P(None, "cols"),
        P("cols", None),
        P(),
        P("batch", "cols"),
        P("cols", "batch"),
        P("batch", "cols"),
        P("batch", "cols"),
        P("batch", "cols"),
        P("cols", "batch"),
        P("batch"),
        P("batch", "cols"),
        P("cols", "batch"),
        P("batch", "cols"),
        P("batch", "cols"),
        P("batch", "cols"),
        P("cols", "batch"),
        P("batch"),
    )
    return jax.shard_map(body, mesh=mesh, in_specs=in_specs, out_specs=out_specs, check_vma=False)
```

profile of v0, /device:TPU:0, one launch (start us, length us, event | category | flops | bytes accessed | tf_op | source)
XLA Modules:
  0.0 326.9 jit_solution(14137713241253828921)
XLA Ops:
  7.2 0.0 reduce-scatter.11.cloned.1.call-start
  7.2 3.8 %convert_bitcast_fusion.1 = bf16[1024,1024]{1,0:T(8,128)(2,1)} fusion(f32[1,1024,1024]{2,1,0:T(8,128)} %param.21), kind=kLoop, calls=%fused_computation.1 | loop fusion | flops 1048576 | bytes 6291456 | tf_op jit(solution)/shard_map/convert_element_type | solution.py:35
  11.1 0.0 reduce-scatter.19.cloned.1.call-start
  11.1 2.5 convert_bitcast_fusion
  13.7 2.6 copy.42
  16.3 0.0 reduce-scatter.13.cloned.1.call-start
  16.3 1.1 copy-done.1
  17.5 0.8 convert_bitcast_fusion.5
  18.3 0.0 reduce-scatter.15.cloned.1.call-start
  18.4 0.8 convert_bitcast_fusion.4
  19.3 0.0 reduce-scatter.17.cloned.1.call-start
  19.3 0.8 convert_bitcast_fusion.3
  20.2 0.0 reduce-scatter.21.cloned.1.call-start
  20.3 0.1 convert_bitcast_fusion.2
  20.3 1.0 copy.44
  21.4 0.0 all-gather.4.cloned.1.call-start
  21.4 34.3 %reduce-scatter.11.cloned.1.call-done = bf16[128,1024]{1,0:T(8,128)(2,1)} async-done(((bf16[1024,1024]{1,0:T(8,128)(2,1)}), bf16[128,1024]{1,0:T(8,128)(2,1)}) %reduce-scatter.11.cloned.1.call-update) | async-done | bytes 262160 | tf_op jit(solution)/shard_map/reduce_scatter | solution.py:34
  55.7 2.1 fusion.5
  57.9 0.0 all-gather.4.cloned.1.call-update
  57.9 0.0 all-gather.6.cloned.1.call-start
  58.0 42.7 %reduce-scatter.19.cloned.1.call-done = bf16[128,1024]{1,0:T(8,128)(2,1)} async-done(((bf16[1024,1024]{1,0:T(8,128)(2,1)}), bf16[128,1024]{1,0:T(8,128)(2,1)}) %reduce-scatter.19.cloned.1.call-update) | async-done | bytes 262160
  100.7 1.1 copy.43
  101.9 1.2 fusion.4
  103.1 12.7 %psum.7 = f32[1024]{0:T(1024)S(1)} all-reduce(f32[1024]{0:T(1024)S(1)} %bitcast.24), channel_id=1, replica_groups=mesh['batch'=8,'cols'=4] {'batch'}, use_global_device_ids=true, to_apply=%region_6.0 | all-reduce | flops 1024 | bytes 8192 | tf_op jit(solution)/shard_map/psum | solution.py:53
  115.8 0.6 convert_bitcast_fusion.6
  116.4 8.7 %all-gather = bf16[8,1,128]{2,1,0:T(2,128)(2,1)S(1)} all-gather(bf16[1,1,128]{2,1,0:T(2,128)(2,1)S(1)} %get-tuple-element.21), channel_id=1, replica_groups=mesh['batch'=8,'cols'=4] {'batch'}, dimensions={0}, use_global_device_ids=true | all-gather | bytes 2304 | tf_op jit(solution)/shard_map/all_gather | solution.py:87
  125.1 0.6 reduce
  125.7 12.8 %reduce-scatter.13.cloned.1.call-done = bf16[128,256]{1,0:T(8,128)(2,1)} async-done(((bf16[1024,256]{1,0:T(8,128)(2,1)}), bf16[128,256]{1,0:T(8,128)(2,1)}) %reduce-scatter.13.cloned.1.call-update) | async-done | bytes 65552 | tf_op jit(solution)/shard_map/reduce_scatter | solution.py:40
  138.5 1.6 fusion.3
  140.1 9.8 %all_gather.23 = bf16[1024,256]{1,0:T(8,128)(2,1)S(1)} all-gather(bf16[128,256]{1,0:T(8,128)(2,1)S(1)} %get-tuple-element.33), channel_id=1, replica_groups=mesh['batch'=8,'cols'=4] {'batch'}, dimensions={0}, use_global_device_ids=true | all-gather | bytes 589824 | tf_op jit(solution)/shard_map/all_gather | solution.py:83
  149.9 26.3 %reduce-scatter.15.cloned.1.call-done = bf16[128,256]{1,0:T(8,128)(2,1)} async-done(((bf16[1024,256]{1,0:T(8,128)(2,1)}), bf16[128,256]{1,0:T(8,128)(2,1)}) %reduce-scatter.15.cloned.1.call-update) | async-done | bytes 65552 | tf_op jit(solution)/shard_map/reduce_scatter | solution.py:43
  176.2 1.6 fusion.2
  177.7 9.8 %all_gather.24 = bf16[1024,256]{1,0:T(8,128)(2,1)S(1)} all-gather(bf16[128,256]{1,0:T(8,128)(2,1)S(1)} %get-tuple-element.30), channel_id=1, replica_groups=mesh['batch'=8,'cols'=4] {'batch'}, dimensions={0}, use_global_device_ids=true | all-gather | bytes 589824 | tf_op jit(solution)/shard_map/all_gather | solution.py:84
  187.5 26.3 %reduce-scatter.17.cloned.1.call-done = bf16[128,256]{1,0:T(8,128)(2,1)} async-done(((bf16[1024,256]{1,0:T(8,128)(2,1)}), bf16[128,256]{1,0:T(8,128)(2,1)}) %reduce-scatter.17.cloned.1.call-update) | async-done | bytes 65552 | tf_op jit(solution)/shard_map/reduce_scatter | solution.py:46
  213.8 1.6 fusion.1
  215.4 9.8 %all_gather.25 = bf16[1024,256]{1,0:T(8,128)(2,1)S(1)} all-gather(bf16[128,256]{1,0:T(8,128)(2,1)S(1)} %get-tuple-element.27), channel_id=1, replica_groups=mesh['batch'=8,'cols'=4] {'batch'}, dimensions={0}, use_global_device_ids=true | all-gather | bytes 589824 | tf_op jit(solution)/shard_map/all_gather | solution.py:85
  225.2 26.3 %reduce-scatter.21.cloned.1.call-done = bf16[128,256]{1,0:T(8,128)(2,1)} async-done(((bf16[1024,256]{1,0:T(8,128)(2,1)}), bf16[128,256]{1,0:T(8,128)(2,1)}) %reduce-scatter.21.cloned.1.call-update) | async-done | bytes 65552
  251.5 0.9 copy.45
  252.5 0.7 fusion
  253.2 9.9 %all_gather.26 = bf16[256,1024]{1,0:T(8,128)(2,1)S(1)} all-gather(bf16[256,128]{1,0:T(8,128)(2,1)S(1)} %get-tuple-element.24), channel_id=1, replica_groups=mesh['batch'=8,'cols'=4] {'batch'}, dimensions={1}, use_global_device_ids=true | all-gather | bytes 589824 | tf_op jit(solution)/shard_map/all_gather | solution.py:86
  263.1 18.7 %all-gather.4.cloned.1.call-done = bf16[1024,1024]{1,0:T(8,128)(2,1)} async-done(((bf16[128,1024]{1,0:T(8,128)(2,1)}), bf16[1024,1024]{1,0:T(8,128)(2,1)}) %all-gather.4.cloned.1.call-update) | async-done | bytes 2097168 | tf_op jit(solution)/shard_map/all_gather | solution.py:81
  281.8 30.6 %all-gather.6.cloned.1.call-done = bf16[1024,1024]{1,0:T(8,128)(2,1)} async-done(((bf16[1024,128]{1,0:T(8,128)(2,1)}), bf16[1024,1024]{1,0:T(8,128)(2,1)}) %all-gather.6.cloned.1.call-update) | async-done | bytes 2097168 | tf_op jit(solution)/shard_map/all_gather | solution.py:82
  312.4 3.2 copy.52
  315.6 1.3 copy.53
  316.9 0.8 copy.54
  317.7 0.8 copy.55
  318.5 0.8 copy.56
  319.3 0.8 copy.57
  (46 shorter events, 0.2 us)
Async XLA Ops:
  7.2 48.5 %reduce-scatter.11.cloned.1.call-start = ((), (), s32[]{:S(2)}) async-start(), calls=%async_computation.6 | async-start | bytes 2359296 | tf_op jit(solution)/shard_map/reduce_scatter | solution.py:34
  11.1 89.6 %reduce-scatter.19.cloned.1.call-start = ((), (), s32[]{:S(2)}) async-start(), calls=%async_computation.12 | async-start | bytes 2359296
  16.2 1.2 copy-start.1
  16.2 2.2 copy-start.2
  16.3 3.1 copy-start.3
  16.3 122.2 %reduce-scatter.13.cloned.1.call-start = ((), (), s32[]{:S(2)}) async-start(), calls=%async_computation.9 | async-start | bytes 589824 | tf_op jit(solution)/shard_map/reduce_scatter | solution.py:40
  18.3 1.9 copy-start.4
  18.3 157.8 %reduce-scatter.15.cloned.1.call-start = ((), (), s32[]{:S(2)}) async-start(), calls=%async_computation.10 | async-start | bytes 589824 | tf_op jit(solution)/shard_map/reduce_scatter | solution.py:43
  19.3 194.6 %reduce-scatter.17.cloned.1.call-start = ((), (), s32[]{:S(2)}) async-start(), calls=%async_computation.11 | async-start | bytes 589824 | tf_op jit(solution)/shard_map/reduce_scatter | solution.py:46
  20.2 35.6 %copy-start.5 = (f32[128,1024]{1,0:T(8,128)S(1)}, f32[128,1024]{1,0:T(8,128)}, u32[]{:S(2)}) copy-start(f32[128,1024]{1,0:T(8,128)} %param.28) | copy-start | bytes 1572868
  20.2 35.6 %copy-start.6 = (f32[128,1024]{1,0:T(8,128)S(1)}, f32[128,1024]{1,0:T(8,128)}, u32[]{:S(2)}) copy-start(f32[128,1024]{1,0:T(8,128)} %param.35) | copy-start | bytes 1572868
  20.2 231.3 %reduce-scatter.21.cloned.1.call-start = ((), (), s32[]{:S(2)}) async-start(), calls=%async_computation.13 | async-start | bytes 589824
  21.3 80.5 %copy-start.7 = (f32[1024,128]{1,0:T(8,128)S(1)}, f32[1024,128]{1,0:T(8,128)}, u32[]{:S(2)}) copy-start(f32[1024,128]{1,0:T(8,128)} %param.29) | copy-start | bytes 1572868
  21.3 80.5 %copy-start.8 = (f32[1024,128]{1,0:T(8,128)S(1)}, f32[1024,128]{1,0:T(8,128)}, u32[]{:S(2)}) copy-start(f32[1024,128]{1,0:T(8,128)} %param.36) | copy-start | bytes 1572868
  21.4 260.4 %all-gather.4.cloned.1.call-start = ((), (), s32[]{:S(2)}) async-start(), calls=%async_computation.7 | async-start | bytes 2359296 | tf_op jit(solution)/shard_map/all_gather | solution.py:81
  57.9 45.2 %copy-start.17 = (f32[1,1024]{1,0:T(1,128)S(1)}, f32[1,1024]{1,0:T(1,128)}, u32[]{:S(2)}) copy-start(f32[1,1024]{1,0:T(1,128)} %param.27) | copy-start | bytes 12292
  57.9 57.9 %copy-start.18 = (f32[128]{0:T(128)S(1)}, f32[128]{0:T(128)}, u32[]{:S(2)}) copy-start(f32[128]{0:T(128)} %param.34) | copy-start | bytes 1540
  57.9 57.9 %copy-start.19 = (f32[128]{0:T(128)S(1)}, f32[128]{0:T(128)}, u32[]{:S(2)}) copy-start(f32[128]{0:T(128)} %param.41) | copy-start | bytes 1540
  57.9 80.6 %copy-start.9 = (f32[128,256]{1,0:T(8,128)S(1)}, f32[128,256]{1,0:T(8,128)}, u32[]{:S(2)}) copy-start(f32[128,256]{1,0:T(8,128)} %param.30) | copy-start | bytes 393220
  57.9 80.6 %copy-start.10 = (f32[128,256]{1,0:T(8,128)S(1)}, f32[128,256]{1,0:T(8,128)}, u32[]{:S(2)}) copy-start(f32[128,256]{1,0:T(8,128)} %param.37) | copy-start | bytes 393220
  57.9 254.4 %all-gather.6.cloned.1.call-start = ((), (), s32[]{:S(2)}) async-start(), calls=%async_computation.8 | async-start | bytes 2359296 | tf_op jit(solution)/shard_map/all_gather | solution.py:82
  101.9 74.3 %copy-start.11 = (f32[128,256]{1,0:T(8,128)S(1)}, f32[128,256]{1,0:T(8,128)}, u32[]{:S(2)}) copy-start(f32[128,256]{1,0:T(8,128)} %param.31) | copy-start | bytes 393220
  101.9 74.3 %copy-start.12 = (f32[128,256]{1,0:T(8,128)S(1)}, f32[128,256]{1,0:T(8,128)}, u32[]{:S(2)}) copy-start(f32[128,256]{1,0:T(8,128)} %param.38) | copy-start | bytes 393220
  101.9 112.0 %copy-start.13 = (f32[128,256]{1,0:T(8,128)S(1)}, f32[128,256]{1,0:T(8,128)}, u32[]{:S(2)}) copy-start(f32[128,256]{1,0:T(8,128)} %param.32) | copy-start | bytes 393220
  101.9 112.0 %copy-start.14 = (f32[128,256]{1,0:T(8,128)S(1)}, f32[128,256]{1,0:T(8,128)}, u32[]{:S(2)}) copy-start(f32[128,256]{1,0:T(8,128)} %param.39) | copy-start | bytes 393220
  103.1 149.4 %copy-start.15 = (f32[256,128]{1,0:T(8,128)S(1)}, f32[256,128]{1,0:T(8,128)}, u32[]{:S(2)}) copy-start(f32[256,128]{1,0:T(8,128)} %param.33) | copy-start | bytes 393220
  103.1 149.4 %copy-start.16 = (f32[256,128]{1,0:T(8,128)S(1)}, f32[256,128]{1,0:T(8,128)}, u32[]{:S(2)}) copy-start(f32[256,128]{1,0:T(8,128)} %param.40) | copy-start | bytes 393220
  312.4 3.2 copy-start
Sparse Core Ops, SparseCore 0:
  11.9 43.8 reduce-scatter.10
  59.6 41.0 reduce-scatter.18
  104.4 34.0 reduce-scatter.12
  142.0 34.1 reduce-scatter.14
  179.7 34.1 reduce-scatter.16
  217.3 34.1 reduce-scatter.20
  254.0 27.7 all-gather.3
  284.2 28.0 all-gather.5
where the time goes:
time: 327 us
  waiting for transfers between devices  218 us (67%)
  blocking collectives  60.6 us (19%)
  other arithmetic  18.9 us (6%)
  local copies, waits for them, and re-layouts  14.6 us (4%)
  between operations  14.4 us (4%)
    unnamed x10, waiting for transfers between devices  69.2 us
    reduce_scatter x1, waiting for transfers between devices, body(): lax.psum_scatter(grad_up[0].astype(jnp.bfloat16), 'batch', scatter_dimens...  34.3 us
    all_gather x1, waiting for transfers between devices, body(): lax.all_gather(new_down.astype(jnp.bfloat16), 'batch', axis=1, tiled=True)  30.6 us
    reduce_scatter x1, waiting for transfers between devices, body(): lax.psum_scatter(grad_key[0].astype(jnp.bfloat16), 'batch', scatter_dimen...  26.3 us
    reduce_scatter x1, waiting for transfers between devices, body(): lax.psum_scatter(grad_value[0].astype(jnp.bfloat16), 'batch', scatter_dim...  26.3 us
    all_gather x1, waiting for transfers between devices, body(): lax.all_gather(new_up.astype(jnp.bfloat16), 'batch', axis=0, tiled=True)  18.7 us
    unnamed x50, local copies, waits for them, and re-layouts  14.6 us
    reduce_scatter x1, waiting for transfers between devices, body(): lax.psum_scatter(grad_query[0].astype(jnp.bfloat16), 'batch', scatter_dim...  12.8 us
  transfers between devices with their start and end apart: 8, of which 8 were waited for; matrix products, arithmetic and copies ran while one was open for 6% of the time, Pallas kernels for 0%

commit v1 on v0

--- a/solution.py
+++ b/solution.py
@@ -5,6 +5,13 @@
 
 learn_rate = 0.1
 hold_rate = 0.7
+
+
+def clusters_build(frame, on_dim):
+    lower = jnp.stack([frame for _ in range(lax.axis_size("batch"))], 0)
+    outer = lax.all_to_all(lower, "batch", 0, 0)
+    latest = jnp.concatenate(outer, on_dim)
+    return latest
 
 
 def body(
@@ -79,7 +86,7 @@
     new_norm = weight_norm - learn_rate * state_new_norm
     copy_up, copy_down, copy_query, copy_key, copy_value, copy_mixed, copy_norm = (
         lax.all_gather(new_up.astype(jnp.bfloat16), "batch", axis=0, tiled=True),
-        lax.all_gather(new_down.astype(jnp.bfloat16), "batch", axis=1, tiled=True),
+        clusters_build(new_down.astype(jnp.bfloat16), 1),
         lax.all_gather(new_query.astype(jnp.bfloat16), "batch", axis=0, tiled=True),
         lax.all_gather(new_key.astype(jnp.bfloat16), "batch", axis=0, tiled=True),
         lax.all_gather(new_value.astype(jnp.bfloat16), "batch", axis=0, tiled=True),

time: 327 us -> 299 us (0.914)
  waiting for transfers between devices: 218 us -> 154 us
  blocking collectives: 60.6 us -> 83.5 us
  local copies, waits for them, and re-layouts: 14.6 us -> 21.2 us
  starting transfers between devices: 0.33 us -> 4.04 us
    all_gather x1 -> x0, waiting for transfers between devices: 30.6 us -> none  [body(): lax.all_gather(new_down.astype(jnp.bfloat16), 'batch', axis=1, tiled=True)]
    psum x1, blocking collectives: 12.7 us -> 34.4 us  [body(): whole_norm = lax.psum(grad_norm[0], 'batch')]
    reduce_scatter x1, waiting for transfers between devices: 12.8 us -> 0.01 us  [body(): lax.psum_scatter(grad_query[0].astype(jnp.bfloat16), 'batch', scatter_dim...]
    reduce_scatter x1, waiting for transfers between devices: 26.3 us -> 16.4 us  [body(): lax.psum_scatter(grad_key[0].astype(jnp.bfloat16), 'batch', scatter_dimen...]
    all_gather x1, waiting for transfers between devices: 18.7 us -> 9.64 us  [body(): lax.all_gather(new_up.astype(jnp.bfloat16), 'batch', axis=0, tiled=True)]
    all_to_all x0 -> x1, starting transfers between devices: none -> 3.75 us  [clusters_build(): outer = lax.all_to_all(lower, 'batch', 0, 0)]
    unnamed x50 -> x48, local copies, waits for them, and re-layouts: 14.6 us -> 17 us
    unnamed x10 -> x9, waiting for transfers between devices: 69.2 us -> 68.3 us
  transfers between devices with their start and end apart: 8 -> 8, of which waited for: 8 -> 6; matrix products, arithmetic and copies ran while one was open for 6% -> 10% of each run, Pallas kernels for 0% -> 0%
where the time goes in v1:
time: 299 us; the launch traced here: 298 us
  waiting for transfers between devices  154 us (52%)
  blocking collectives  83.5 us (28%)
  local copies, waits for them, and re-layouts  21.2 us (7%)
  other arithmetic  21.1 us (7%)
  between operations  14.3 us (5%)
  starting transfers between devices  4.04 us (1%)
    unnamed x9, waiting for transfers between devices  68.3 us
    psum x1, blocking collectives, body(): whole_norm = lax.psum(grad_norm[0], 'batch')  34.4 us
    reduce_scatter x1, waiting for transfers between devices, body(): lax.psum_scatter(grad_up[0].astype(jnp.bfloat16), 'batch', scatter_dimens...  33 us
    reduce_scatter x1, waiting for transfers between devices, body(): lax.psum_scatter(grad_value[0].astype(jnp.bfloat16), 'batch', scatter_dim...  26.3 us
    unnamed x48, local copies, waits for them, and re-layouts  17 us
    reduce_scatter x1, waiting for transfers between devices, body(): lax.psum_scatter(grad_key[0].astype(jnp.bfloat16), 'batch', scatter_dimen...  16.4 us
    all_gather x1, blocking collectives, body(): lax.all_gather(new_mixed.astype(jnp.bfloat16), 'batch', axis=1, tiled=True)  10.9 us
    all_gather x1, blocking collectives, body(): lax.all_gather(new_value.astype(jnp.bfloat16), 'batch', axis=0, tiled=True)  10.7 us
  transfers between devices with their start and end apart: 8, of which 6 were waited for; matrix products, arithmetic and copies ran while one was open for 10% of the time, Pallas kernels for 0%

profile of v1, /device:TPU:0, one launch (start us, length us, event | category | flops | bytes accessed | tf_op | source)
XLA Modules:
  0.0 297.8 jit_solution(17572315925445467419)
XLA Ops:
  7.2 0.0 reduce-scatter.11.cloned.1.call-start
  7.2 3.8 %convert_bitcast_fusion.1 = bf16[1024,1024]{1,0:T(8,128)(2,1)} fusion(f32[1,1024,1024]{2,1,0:T(8,128)} %param.21), kind=kLoop, calls=%fused_computation.1 | loop fusion | flops 1048576 | bytes 6291456 | tf_op jit(solution)/shard_map/convert_element_type | solution.py:42
  11.1 0.0 reduce-scatter.11.cloned.1.call-update
  11.1 0.0 reduce-scatter.19.cloned.1.call-start
  11.1 2.5 convert_bitcast_fusion
  13.7 2.6 copy.44
  16.3 0.0 reduce-scatter.13.cloned.1.call-start
  16.3 1.1 copy-done.2
  17.5 0.8 convert_bitcast_fusion.5
  18.3 0.0 reduce-scatter.15.cloned.1.call-start
  18.4 0.8 convert_bitcast_fusion.4
  19.3 0.0 reduce-scatter.17.cloned.1.call-start
  19.3 0.8 convert_bitcast_fusion.3
  20.2 0.0 reduce-scatter.21.cloned.1.call-start
  20.2 1.4 convert_bitcast_fusion.2
  21.6 1.0 copy.46
  22.7 0.0 all-gather.3.cloned.1.call-start
  22.7 33.0 %reduce-scatter.11.cloned.1.call-done = bf16[128,1024]{1,0:T(8,128)(2,1)} async-done(((bf16[1024,1024]{1,0:T(8,128)(2,1)}), bf16[128,1024]{1,0:T(8,128)(2,1)}) %reduce-scatter.11.cloned.1.call-update) | async-done | bytes 262160 | tf_op jit(solution)/shard_map/reduce_scatter | solution.py:41
  55.7 2.1 fusion.5
  57.9 42.8 %reduce-scatter.19.cloned.1.call-done = bf16[128,1024]{1,0:T(8,128)(2,1)} async-done(((bf16[1024,1024]{1,0:T(8,128)(2,1)}), bf16[128,1024]{1,0:T(8,128)(2,1)}) %reduce-scatter.19.cloned.1.call-update) | async-done | bytes 262160
  100.7 1.1 copy.45
  101.9 1.1 fusion.4
  103.0 1.6 stack.2
  104.6 3.7 %all-to-all-start = ((bf16[8,1024,128]{2,1,0:T(8,128)(2,1)}), bf16[8,1024,128]{2,1,0:T(8,128)(2,1)S(1)}, u32[]{:S(2)}, u32[]{:S(2)}) async-start(bf16[8,1024,128]{2,1,0:T(8,128)(2,1)} %stack.2), calls=%async_computation.1 | async-start | bytes 4194304 | tf_op jit(solution)/shard_map/all_to_all | solution.py:12
  108.4 34.4 %psum.7 = f32[1024]{0:T(1024)S(1)} all-reduce(f32[1024]{0:T(1024)S(1)} %bitcast.28), channel_id=1, replica_groups=mesh['batch'=8,'cols'=4] {'batch'}, use_global_device_ids=true, to_apply=%region_6.0 | all-reduce | flops 1024 | bytes 8192 | tf_op jit(solution)/shard_map/psum | solution.py:60
  142.8 0.6 convert_bitcast_fusion.6
  143.4 8.9 %all-gather = bf16[8,1,128]{2,1,0:T(2,128)(2,1)S(1)} all-gather(bf16[1,1,128]{2,1,0:T(2,128)(2,1)S(1)} %get-tuple-element.42), channel_id=1, replica_groups=mesh['batch'=8,'cols'=4] {'batch'}, dimensions={0}, use_global_device_ids=true | all-gather | bytes 2304 | tf_op jit(solution)/shard_map/all_gather | solution.py:94
  152.4 0.6 reduce
  153.0 1.6 fusion.3
  154.5 8.7 %all_gather.19 = bf16[1024,256]{1,0:T(8,128)(2,1)S(1)} all-gather(bf16[128,256]{1,0:T(8,128)(2,1)S(1)} %get-tuple-element.54), channel_id=1, replica_groups=mesh['batch'=8,'cols'=4] {'batch'}, dimensions={0}, use_global_device_ids=true | all-gather | bytes 589824 | tf_op jit(solution)/shard_map/all_gather | solution.py:90
  163.2 16.4 %reduce-scatter.15.cloned.1.call-done = bf16[128,256]{1,0:T(8,128)(2,1)} async-done(((bf16[1024,256]{1,0:T(8,128)(2,1)}), bf16[128,256]{1,0:T(8,128)(2,1)}) %reduce-scatter.15.cloned.1.call-update) | async-done | bytes 65552 | tf_op jit(solution)/shard_map/reduce_scatter | solution.py:50
  179.7 1.6 fusion.2
  181.2 9.8 %all_gather.20 = bf16[1024,256]{1,0:T(8,128)(2,1)S(1)} all-gather(bf16[128,256]{1,0:T(8,128)(2,1)S(1)} %get-tuple-element.51), channel_id=1, replica_groups=mesh['batch'=8,'cols'=4] {'batch'}, dimensions={0}, use_global_device_ids=true | all-gather | bytes 589824 | tf_op jit(solution)/shard_map/all_gather | solution.py:91
  191.0 26.3 %reduce-scatter.17.cloned.1.call-done = bf16[128,256]{1,0:T(8,128)(2,1)} async-done(((bf16[1024,256]{1,0:T(8,128)(2,1)}), bf16[128,256]{1,0:T(8,128)(2,1)}) %reduce-scatter.17.cloned.1.call-update) | async-done | bytes 65552 | tf_op jit(solution)/shard_map/reduce_scatter | solution.py:53
  217.3 1.6 fusion.1
  218.9 10.7 %all_gather.21 = bf16[1024,256]{1,0:T(8,128)(2,1)} all-gather(bf16[128,256]{1,0:T(8,128)(2,1)S(1)} %get-tuple-element.48), channel_id=1, replica_groups=mesh['batch'=8,'cols'=4] {'batch'}, dimensions={0}, use_global_device_ids=true | all-gather | bytes 589824 | tf_op jit(solution)/shard_map/all_gather | solution.py:92
  229.6 25.3 %reduce-scatter.21.cloned.1.call-done = bf16[128,256]{1,0:T(8,128)(2,1)} async-done(((bf16[1024,256]{1,0:T(8,128)(2,1)}), bf16[128,256]{1,0:T(8,128)(2,1)}) %reduce-scatter.21.cloned.1.call-update) | async-done | bytes 65552
  255.0 0.9 copy.47
  255.9 1.6 fusion
  257.6 10.9 %all_gather.22 = bf16[256,1024]{1,0:T(8,128)(2,1)} all-gather(bf16[256,128]{1,0:T(8,128)(2,1)S(1)} %get-tuple-element.45), channel_id=1, replica_groups=mesh['batch'=8,'cols'=4] {'batch'}, dimensions={1}, use_global_device_ids=true | all-gather | bytes 589824 | tf_op jit(solution)/shard_map/all_gather | solution.py:93
  268.5 2.6 copy.42
  271.1 3.9 %copy.43 = bf16[1024,1024]{1,0:T(8,128)(2,1)} copy(bf16[1024,1024]{0,1:T(8,128)(2,1)} %bitcast.24) | data formatting | bytes 4194304
  275.0 9.6 %all-gather.3.cloned.1.call-done = bf16[1024,1024]{1,0:T(8,128)(2,1)} async-done(((bf16[128,1024]{1,0:T(8,128)(2,1)}), bf16[1024,1024]{1,0:T(8,128)(2,1)}) %all-gather.3.cloned.1.call-update) | async-done | bytes 2097168 | tf_op jit(solution)/shard_map/all_gather | solution.py:88
  284.7 3.1 %copy.53 = bf16[1024,1024]{1,0:T(8,128)(2,1)} copy(bf16[1024,1024]{1,0:T(8,128)(2,1)} %all-gather.3.cloned.1.call-done) | data formatting | bytes 4194304
  287.8 0.8 copy.54
  288.6 0.8 copy.55
  289.4 0.8 copy.56
  290.2 0.8 copy.57
  (45 shorter events, 0.2 us)
Async XLA Ops:
  7.2 48.5 %reduce-scatter.11.cloned.1.call-start = ((), (), s32[]{:S(2)}) async-start(), calls=%async_computation.7 | async-start | bytes 2359296 | tf_op jit(solution)/shard_map/reduce_scatter | solution.py:41
  11.1 89.6 %reduce-scatter.19.cloned.1.call-start = ((), (), s32[]{:S(2)}) async-start(), calls=%async_computation.12 | async-start | bytes 2359296
  16.2 1.2 copy-start.2
  16.2 2.1 copy-start.3
  16.3 3.0 %copy-start.4 = (f32[1,1024,256]{2,1,0:T(8,128)S(1)}, f32[1,1024,256]{2,1,0:T(8,128)}, u32[]{:S(2)}) copy-start(f32[1,1024,256]{2,1,0:T(8,128)} %param.25) | copy-start | bytes 3145732
  16.3 136.7 %reduce-scatter.13.cloned.1.call-start = ((), (), s32[]{:S(2)}) async-start(), calls=%async_computation.9 | async-start | bytes 589824 | tf_op jit(solution)/shard_map/reduce_scatter | solution.py:47
  18.3 161.3 %reduce-scatter.15.cloned.1.call-start = ((), (), s32[]{:S(2)}) async-start(), calls=%async_computation.10 | async-start | bytes 589824 | tf_op jit(solution)/shard_map/reduce_scatter | solution.py:50
  19.3 198.1 %reduce-scatter.17.cloned.1.call-start = ((), (), s32[]{:S(2)}) async-start(), calls=%async_computation.11 | async-start | bytes 589824 | tf_op jit(solution)/shard_map/reduce_scatter | solution.py:53
  20.2 35.6 %copy-start.5 = (f32[128,1024]{1,0:T(8,128)S(1)}, f32[128,1024]{1,0:T(8,128)}, u32[]{:S(2)}) copy-start(f32[128,1024]{1,0:T(8,128)} %param.28) | copy-start | bytes 1572868
  20.2 35.6 %copy-start.6 = (f32[128,1024]{1,0:T(8,128)S(1)}, f32[128,1024]{1,0:T(8,128)}, u32[]{:S(2)}) copy-start(f32[128,1024]{1,0:T(8,128)} %param.35) | copy-start | bytes 1572868
  20.2 234.8 %reduce-scatter.21.cloned.1.call-start = ((), (), s32[]{:S(2)}) async-start(), calls=%async_computation.13 | async-start | bytes 589824
  22.6 79.2 %copy-start.7 = (f32[1024,128]{1,0:T(8,128)S(1)}, f32[1024,128]{1,0:T(8,128)}, u32[]{:S(2)}) copy-start(f32[1024,128]{1,0:T(8,128)} %param.29) | copy-start | bytes 1572868
  22.6 79.2 %copy-start.8 = (f32[1024,128]{1,0:T(8,128)S(1)}, f32[1024,128]{1,0:T(8,128)}, u32[]{:S(2)}) copy-start(f32[1024,128]{1,0:T(8,128)} %param.36) | copy-start | bytes 1572868
  22.7 262.0 %all-gather.3.cloned.1.call-start = ((), (), s32[]{:S(2)}) async-start(), calls=%async_computation.8 | async-start | bytes 2359296 | tf_op jit(solution)/shard_map/all_gather | solution.py:88
  104.6 3.8 %copy-start.16 = (f32[1,1024]{1,0:T(1,128)S(1)}, f32[1,1024]{1,0:T(1,128)}, u32[]{:S(2)}) copy-start(f32[1,1024]{1,0:T(1,128)} %param.27) | copy-start | bytes 12292
  104.6 38.3 %copy-start.17 = (f32[128]{0:T(128)S(1)}, f32[128]{0:T(128)}, u32[]{:S(2)}) copy-start(f32[128]{0:T(128)} %param.34) | copy-start | bytes 1540
  104.6 38.3 %copy-start.18 = (f32[128]{0:T(128)S(1)}, f32[128]{0:T(128)}, u32[]{:S(2)}) copy-start(f32[128]{0:T(128)} %param.41) | copy-start | bytes 1540
  104.6 48.4 %copy-start.9 = (f32[128,256]{1,0:T(8,128)S(1)}, f32[128,256]{1,0:T(8,128)}, u32[]{:S(2)}) copy-start(f32[128,256]{1,0:T(8,128)} %param.30) | copy-start | bytes 393220
  104.6 48.4 %copy-start.10 = (f32[128,256]{1,0:T(8,128)S(1)}, f32[128,256]{1,0:T(8,128)}, u32[]{:S(2)}) copy-start(f32[128,256]{1,0:T(8,128)} %param.37) | copy-start | bytes 393220
  104.6 75.1 %copy-start.11 = (f32[128,256]{1,0:T(8,128)S(1)}, f32[128,256]{1,0:T(8,128)}, u32[]{:S(2)}) copy-start(f32[128,256]{1,0:T(8,128)} %param.31) | copy-start | bytes 393220
  104.6 75.1 %copy-start.12 = (f32[128,256]{1,0:T(8,128)S(1)}, f32[128,256]{1,0:T(8,128)}, u32[]{:S(2)}) copy-start(f32[128,256]{1,0:T(8,128)} %param.38) | copy-start | bytes 393220
  104.6 163.9 %all-to-all-start = ((bf16[8,1024,128]{2,1,0:T(8,128)(2,1)}), bf16[8,1024,128]{2,1,0:T(8,128)(2,1)S(1)}, u32[]{:S(2)}, u32[]{:S(2)}) async-start(bf16[8,1024,128]{2,1,0:T(8,128)(2,1)} %stack.2), calls=%async_computation.1 | async-start | bytes 4194304 | tf_op jit(solution)/shard_map/all_to_all | solution.py:12
  108.4 109.0 %copy-start.13 = (f32[128,256]{1,0:T(8,128)S(1)}, f32[128,256]{1,0:T(8,128)}, u32[]{:S(2)}) copy-start(f32[128,256]{1,0:T(8,128)} %param.32) | copy-start | bytes 393220
  108.4 108.9 %copy-start.14 = (f32[128,256]{1,0:T(8,128)S(1)}, f32[128,256]{1,0:T(8,128)}, u32[]{:S(2)}) copy-start(f32[128,256]{1,0:T(8,128)} %param.39) | copy-start | bytes 393220
  108.4 147.6 %copy-start.15 = (f32[256,128]{1,0:T(8,128)S(1)}, f32[256,128]{1,0:T(8,128)}, u32[]{:S(2)}) copy-start(f32[256,128]{1,0:T(8,128)} %param.33) | copy-start | bytes 393220
  287.8 1.6 copy-start
  287.8 2.4 copy-start.1
Sparse Core Ops, SparseCore 0:
  11.9 43.8 reduce-scatter.10
  59.6 41.0 reduce-scatter.18
  104.4 37.5 reduce-scatter.12
  145.5 34.0 reduce-scatter.14
  183.1 34.1 reduce-scatter.16
  220.8 34.1 reduce-scatter.20
  256.9 27.7 all-gather.2
